TPU v7x, 32 devices: a whole 2x2x4 slice. The times are simulated.
32 devices in a mesh: row: 8 (over y, x, core), col: 4 (over z).
Axes of the slice: x: 2, y: 2, z: 4, core: 2. Of those that a mesh axis runs over, the one named last changes fastest.
Arguments:
- vectors: float32 [32768, 4096], P('row', 'col'), may hold values from -6 to 6
- reflectors: float32 [8, 32768, 128], P('col', 'row'), may hold values from -0.03125 to 0.03125
- triangles: float32 [8, 128, 128], P('col'), may hold values from -0.25 to 1.8, as said below
Outputs:
- transformed: float32 [32768, 4096], P('row', 'col')
Inputs may be any that keep to these rules, and one draw needn't show every extreme that they name: Each triangles[p] is upper triangular with diagonal entries between 0.5 and 1.8.
All inputs are finite; a program needn't handle non-finite values.
Results may differ from a plain program's by a relative error of at most 0.00013.
Values sent between devices are 32-bit elements; how exact they have to be, the bound alone decides.
A program may use at most 128 MiB of HBM per device.

v0:
```python
import jax
import jax.numpy as jnp
from jax import lax
from jax.sharding import PartitionSpec as P

FULL = lax.Precision.HIGHEST
THREE = lax.Precision.HIGH


def product_t(left, right, precision=THREE):
    return lax.dot_general(
        left,
        right,
        (((0,), (0,)), ((), ())),
        precision=precision,
        preferred_element_type=jnp.float32,
    )


def matmul(left, right, precision=THREE):
    return jnp.dot(left, right, precision=precision, preferred_element_type=jnp.float32)


def merge(tri_a, inner, tri_b):
    coupling = -matmul(matmul(tri_a, inner, FULL), tri_b, FULL)
    zero = jnp.zeros((tri_b.shape[0], tri_a.shape[1]), jnp.float32)
    return jnp.concatenate(
        [
            jnp.concatenate([tri_a, coupling], axis=1),
            jnp.concatenate([zero, tri_b], axis=1),
        ],
        axis=0,
    )


def after(value, earlier):
    return value + 0.0 * sum(array[0, 0] for array in earlier)


def ring_gather(panels, n):
    up = [(i, (i + 1) % n) for i in range(n)]
    down = [(i, (i - 1) % n) for i in range(n)]
    count = len(panels)
    near = {0: list(panels)}
    lower, upper = list(panels), list(panels)
    for step in range(1, (n - 1) // 2 + 1):
        lower = [lax.ppermute(lower[i], "col", up) for i in range(count)]
        upper = [lax.ppermute(upper[i], "col", down) for i in reversed(range(count))][::-1]
        near[n - step] = lower
        near[step] = upper
    if n % 2 == 0:
        half = (count + 1) // 2
        near[n // 2] = [lax.ppermute(lower[i], "col", up) for i in range(half)] + [
            lax.ppermute(upper[i], "col", down) for i in range(half, count)
        ]
    return near


def shards(vectors, reflectors, triangles):
    per_dev, _, nb = reflectors.shape
    n = lax.axis_size("col")
    rows = lax.axis_size("row")
    me = lax.axis_index("col")
    width = per_dev * nb

    near = ring_gather([reflectors[i] for i in range(per_dev)], n)
    basis = {r: jnp.concatenate(near[r], axis=1) for r in range(n)}

    summed = {}
    summed[0], inner = lax.psum((product_t(basis[0], vectors), product_t(basis[0], basis[0], FULL)), "row")
    tri = triangles[0]
    for i in range(1, per_dev):
        tri = merge(tri, inner[: i * nb, i * nb : (i + 1) * nb], triangles[i])

    last = n // 2
    pairs = []
    for d in range(1, n // 2 + 1):
        low, high = (-(d // 2)) % n, (d - d // 2) % n
        pairs.append(product_t(basis[low], basis[high], FULL))
    share = width // rows
    mine = [lax.dynamic_slice_in_dim(tri, lax.axis_index("row") * share, share, 0)]
    if pairs:
        split = lax.psum_scatter(jnp.stack(pairs), "row", scatter_dimension=1, tiled=True)
        mine += [split[i] for i in range(len(pairs))]
    shared = lax.all_gather(jnp.stack(mine), ("col", "row"), axis=0)
    shared = shared.reshape(n, rows, len(mine), share, width)
    shared = shared.transpose(0, 2, 1, 3, 4).reshape(n, len(mine), width, width)

    def inner_of(i, j):
        ahead = j - i
        d = min(ahead, n - ahead)
        if ahead == d:
            return shared[(i + d // 2) % n, d]
        return shared[(j + d // 2) % n, d].T

    tris = [(i, i + 1, shared[i, 0]) for i in range(n)]
    while len(tris) > 1:
        merged = []
        for a, b in zip(tris[::2], tris[1::2]):
            inner_ab = jnp.concatenate(
                [jnp.concatenate([inner_of(i, j) for j in range(b[0], b[1])], axis=1) for i in range(a[0], a[1])],
                axis=0,
            )
            merged.append((a[0], b[1], merge(a[2], inner_ab, b[2])))
        if len(tris) % 2:
            merged.append(tris[-1])
        tris = merged
    whole = tris[0][2].reshape(n, width, n, width)
    whole = lax.dynamic_slice_in_dim(jnp.concatenate([whole, whole], axis=0), me, n, 0)
    whole = whole.transpose(2, 0, 1, 3)
    whole = lax.dynamic_slice_in_dim(jnp.concatenate([whole, whole], axis=0), me, n, 0)
    columns = [whole[r].reshape(n * width, width) for r in range(n)]

    early = [r for r in range(1, n) if r != last]
    if early:
        joined = product_t(jnp.concatenate([basis[r] for r in early], axis=1), vectors)
        joined = lax.psum(after(joined, [summed[0], inner] + pairs), "row")
        for at, r in enumerate(early):
            summed[r] = joined[at * width : (at + 1) * width]
    order = [0] + early
    scaled = matmul(
        jnp.concatenate([columns[r] for r in order], axis=1),
        jnp.concatenate([summed[r] for r in order], axis=0),
    )
    if n > 1:
        done = [summed[early[-1]] if early else summed[0]]
        summed[last] = lax.psum(after(product_t(basis[last], vectors), done), "row")
        scaled = scaled + matmul(columns[last], summed[last])
    return vectors - matmul(jnp.concatenate([basis[r] for r in range(n)], axis=1), scaled)


def solution(mesh):
    placed = (P("row", "col"), P("col", "row", None), P("col", None, None))
    return jax.shard_map(
        shards, mesh=mesh, in_specs=placed, out_specs=P("row", "col"), check_vma=False
    )
```

profile of v0, /device:TPU:0, one launch (start us, length us, event | category | flops | bytes accessed | tf_op | source)
XLA Modules:
  0.0 486.1 jit_solution(1574006051985618780)
XLA Ops:
  6.5 3.8 slice_bitcast_fusion
  10.3 5.1 %collective-permute-start = (f32[4096,128]{1,0:T(8,128)}, f32[4096,128]{1,0:T(8,128)}, u32[]{:S(2)}, u32[]{:S(2)}) collective-permute-start(f32[4096,128]{1,0:T(8,128)} %get-tuple-element.12), channel_id=1, source_target_pairs={{0,3},{1,0},{2,1},{3,2},{4,7},{5,4},{6,5},{7,6},{8,11},{9,8},{10,9... | collective-permute-start | bytes 6291464 | tf_op jit(solution)/shard_map/ppermute | solution.py:48
  15.4 3.8 collective-permute-start.1
  19.3 11.7 %fusion.29 = f32[256,1024]{1,0:T(8,128)} fusion(f32[4096,1024]{1,0:T(8,128)} %param.3, f32[4096,128]{1,0:T(8,128)S(1)} %get-tuple-element.11, f32[4096,128]{1,0:T(8,128)} %get-tuple-element.12), kind=kOutput, calls=%fused_computation.37 | convolution fusion | flops 6443499520 | bytes 22020096 | tf_op jit(solution)/shard_map/dot_general | solution.py:11
  31.0 9.7 %fusion.31 = f32[256,256]{1,0:T(8,128)} fusion(f32[4096,128]{1,0:T(8,128)S(1)} %get-tuple-element.11, f32[4096,128]{1,0:T(8,128)} %get-tuple-element.12), kind=kOutput, calls=%fused_computation.39 | convolution fusion | flops 3222274048 | bytes 4456448 | tf_op jit(solution)/shard_map/dot_general | solution.py:11
  41.0 3.3 constant_dynamic-update-slice_fusion.7
  45.8 54.5 %all-reduce.13.cloned.1.call-done = (f32[256,256]{1,0:T(8,128)}, f32[256,1024]{1,0:T(8,128)}) async-done(((f32[256,256]{1,0:T(8,128)}, f32[256,1024]{1,0:T(8,128)}), (f32[256,256]{1,0:T(8,128)}, f32[256,1024]{1,0:T(8,128)})) %all-reduce.13.cloned.1.call-update) | async-done | bytes 1310736 | tf_op jit(solution)/shard_map/psum | solution.py:70
  104.1 3.2 constant_dynamic-update-slice_fusion.9
  107.3 44.3 %collective-permute-done.1 = f32[4096,128]{1,0:T(8,128)} collective-permute-done((f32[4096,128]{1,0:T(8,128)S(1)}, f32[4096,128]{1,0:T(8,128)}, u32[]{:S(2)}, u32[]{:S(2)}) %collective-permute-start.1) | collective-permute-done | bytes 2097184 | tf_op jit(solution)/shard_map/ppermute | solution.py:48
  151.6 3.2 constant_dynamic-update-slice_fusion.8
  154.8 8.3 %fusion.30 = f32[256,256]{1,0:T(8,128)S(1)} fusion(f32[4096,256]{1,0:T(8,128)S(1)} %get-tuple-element.21, f32[4096,128]{1,0:T(8,128)S(1)} %get-tuple-element.11, f32[4096,128]{1,0:T(8,128)} %get-tuple-element.12), kind=kOutput, calls=%fused_computation.38 | convolution fusion | flops 3222274048 | bytes 8650752 | tf_op jit(solution)/shard_map/dot_general | solution.py:11
  163.6 32.8 %collective-permute-done.5 = f32[4096,128]{1,0:T(8,128)} collective-permute-done((f32[4096,128]{1,0:T(8,128)S(1)}, f32[4096,128]{1,0:T(8,128)}, u32[]{:S(2)}, u32[]{:S(2)}) %collective-permute-start.5) | collective-permute-done | bytes 2097184 | tf_op jit(solution)/shard_map/ppermute | solution.py:47
  196.4 9.4 %fusion.11 = f32[256,256]{1,0:T(8,128)S(1)} fusion(f32[4096,256]{1,0:T(8,128)S(1)} %get-tuple-element.21, f32[4096,128]{1,0:T(8,128)} %collective-permute-done.5, f32[4096,128]{1,0:T(8,128)} %collective-permute-done.2), kind=kOutput, calls=%fused_computation.19 | convolution fusion | flops 3222274048 | bytes 8650752 | tf_op jit(solution)/shard_map/dot_general | solution.py:11
  208.4 20.0 %fusion.32 = f32[512,1024]{1,0:T(8,128)} fusion(f32[4096,1024]{1,0:T(8,128)} %param.3, f32[4096,128]{1,0:T(8,128)} %collective-permute-done.5, f32[4096,128]{1,0:T(8,128)} %collective-permute-done.2, f32[4096,128]{1,0:T(8,128)} %collective-permute-done.1, f32[4096,128]{1,0:T(8,128)} %collective-permute-done, f32[]{:T(128)} %bitcast.22), kind=kOutput, calls=%fused_computation.42 | convolution fusion | flops 12891717632 | bytes 27262980 | tf_op jit(solution)/shard_map/dot_general | solution.py:11
  230.4 10.3 %reduce-scatter.2.cloned.1.call-done = f32[2,32,256]{2,1,0:T(8,128)} async-done(((f32[2,256,256]{2,1,0:T(8,128)}), f32[2,32,256]{2,1,0:T(8,128)}) %reduce-scatter.2.cloned.1.call-update) | async-done | bytes 65552 | tf_op jit(solution)/shard_map/reduce_scatter | solution.py:83
  243.9 2.5 collective-permute-start.4
  246.4 59.5 %all-reduce.9.cloned.1.call-done = f32[512,1024]{1,0:T(8,128)} async-done(((f32[512,1024]{1,0:T(8,128)}), f32[512,1024]{1,0:T(8,128)}) %all-reduce.9.cloned.1.call-update) | async-done | bytes 2097168 | tf_op jit(solution)/shard_map/psum | solution.py:117
  307.7 30.3 %collective-permute-done.4 = f32[4096,128]{1,0:T(8,128)} collective-permute-done((f32[4096,128]{1,0:T(8,128)}, f32[4096,128]{1,0:T(8,128)}, u32[]{:S(2)}, u32[]{:S(2)}) %collective-permute-start.4) | collective-permute-done | bytes 2097184 | tf_op jit(solution)/shard_map/ppermute | solution.py:54
  338.0 11.8 %fusion.35 = f32[256,1024]{1,0:T(8,128)} fusion(f32[4096,1024]{1,0:T(8,128)} %param.3, f32[4096,128]{1,0:T(8,128)} %collective-permute-done.4, f32[4096,128]{1,0:T(8,128)S(1)} %collective-permute-done.3, f32[]{:T(128)} %bitcast.23), kind=kOutput, calls=%fused_computation.44 | convolution fusion | flops 6443761664 | bytes 22020100 | tf_op jit(solution)/shard_map/dot_general | solution.py:11
  351.3 3.1 constant_dynamic-update-slice_fusion.2
  354.4 3.1 constant_dynamic-update-slice_fusion.1
  357.5 3.1 constant_dynamic-update-slice_fusion
  360.6 16.2 %all-gather.3.cloned.1.call-done = f32[96,32,256]{2,1,0:T(8,128)} async-done(((f32[3,32,256]{2,1,0:T(8,128)}), f32[96,32,256]{2,1,0:T(8,128)}) %all-gather.3.cloned.1.call-update) | async-done | bytes 3145744 | tf_op jit(solution)/shard_map/all_gather | solution.py:85
  387.8 2.3 convolution_negate_fusion.1
  394.4 3.2 fusion.38
  399.5 2.5 select_maximum_fusion
  402.0 5.8 %reshape.18 = f32[4,256,4,256]{1,0,3,2:T(4,128)} reshape(f32[1024,1024]{0,1:T(8,128)} %select_maximum_fusion) | data formatting | bytes 8388608 | tf_op jit(solution)/shard_map/reshape | solution.py:108
  407.8 6.5 %fusion.10 = f32[4,4,256,256]{2,1,3,0:T(4,128)S(1)} fusion(s32[]{:T(128)S(6)} %select_n.8, f32[4,256,4,256]{1,0,3,2:T(4,128)} %reshape.18), kind=kLoop, calls=%fused_computation.15 | loop fusion | flops 1048576 | bytes 8388612 | tf_op jit(solution)/shard_map/transpose | solution.py:110
  418.3 17.0 %all-reduce.11.cloned.1.call-done = f32[256,1024]{1,0:T(8,128)} async-done(((f32[256,1024]{1,0:T(8,128)}), f32[256,1024]{1,0:T(8,128)}) %all-reduce.11.cloned.1.call-update) | async-done | bytes 1048592 | tf_op jit(solution)/shard_map/psum | solution.py:127
  435.3 3.2 fusion.80
  438.6 6.7 %fusion.20 = f32[1024,1024]{1,0:T(8,128)} fusion(f32[1024,256]{0,1:T(8,128)S(1)} %bitcast.111, f32[1024,256]{0,1:T(8,128)S(1)} %bitcast.110, f32[1024,256]{0,1:T(8,128)S(1)} %bitcast.109, f32[512,1024]{1,0:T(8,128)S(1)} %copy-done.5, f32[256,1024]{1,0:T(8,128)S(1)} %copy-done.6), kind=kOutput, calls=%fused_computation.28 | convolution fusion | flops 4834197504 | bytes 10485760 | tf_op jit(solution)/shard_map/dot_general | solution.py:21
  445.3 33.8 %convolution_subtract_fusion = f32[4096,1024]{1,0:T(8,128)} fusion(f32[4096,1024]{1,0:T(8,128)} %param.3, f32[4096,1024]{1,0:T(8,128)} %constant_dynamic-update-slice_fusion, f32[1024,1024]{1,0:T(8,128)} %fusion.20, f32[1024,1024]{1,0:T(8,128)S(1)} %fusion.80), kind=kOutput, calls=%fused_computation.12 | convolution fusion | flops 25775046656 | bytes 58720256 | tf_op jit(solution)/shard_map/dot_general | solution.py:21
  (65 shorter events, 35.1 us)
Async XLA Ops:
  6.5 93.7 %all-reduce.13.cloned.1.call-start = ((), (), s32[]{:S(2)}) async-start(), calls=%async_computation.5 | async-start | bytes 2621440 | tf_op jit(solution)/shard_map/psum | solution.py:70
  10.3 93.7 %collective-permute-start = (f32[4096,128]{1,0:T(8,128)}, f32[4096,128]{1,0:T(8,128)}, u32[]{:S(2)}, u32[]{:S(2)}) collective-permute-start(f32[4096,128]{1,0:T(8,128)} %get-tuple-element.12), channel_id=1, source_target_pairs={{0,3},{1,0},{2,1},{3,2},{4,7},{5,4},{6,5},{7,6},{8,11},{9,8},{10,9... | collective-permute-start | bytes 6291464 | tf_op jit(solution)/shard_map/ppermute | solution.py:48
  15.4 148.2 %collective-permute-start.2 = (f32[4096,128]{1,0:T(8,128)}, f32[4096,128]{1,0:T(8,128)}, u32[]{:S(2)}, u32[]{:S(2)}) collective-permute-start(f32[4096,128]{1,0:T(8,128)} %get-tuple-element.12), channel_id=1, source_target_pairs={{0,1},{1,2},{2,3},{3,0},{4,5},{5,6},{6,7},{7,4},{8,9},{9,10},{10,1... | collective-permute-start | bytes 6291464 | tf_op jit(solution)/shard_map/ppermute | solution.py:47
  15.4 136.2 %collective-permute-start.1 = (f32[4096,128]{1,0:T(8,128)S(1)}, f32[4096,128]{1,0:T(8,128)}, u32[]{:S(2)}, u32[]{:S(2)}) collective-permute-start(f32[4096,128]{1,0:T(8,128)S(1)} %get-tuple-element.11), channel_id=1, source_target_pairs={{0,3},{1,0},{2,1},{3,2},{4,7},{5,4},{6,5},{7,6},{8,11},{9,8},{10,9... | collective-permute-start | bytes 6291464 | tf_op jit(solution)/shard_map/ppermute | solution.py:48
  19.3 177.2 %collective-permute-start.5 = (f32[4096,128]{1,0:T(8,128)S(1)}, f32[4096,128]{1,0:T(8,128)}, u32[]{:S(2)}, u32[]{:S(2)}) collective-permute-start(f32[4096,128]{1,0:T(8,128)S(1)} %get-tuple-element.11), channel_id=1, source_target_pairs={{0,1},{1,2},{2,3},{3,0},{4,5},{5,6},{6,7},{7,4},{8,9},{9,10},{10,1... | collective-permute-start | bytes 6291464 | tf_op jit(solution)/shard_map/ppermute | solution.py:47
  40.7 200.1 %reduce-scatter.2.cloned.1.call-start = ((), (), s32[]{:S(2)}) async-start(), calls=%async_computation.1 | async-start | bytes 589824 | tf_op jit(solution)/shard_map/reduce_scatter | solution.py:83
  41.0 3.3 copy-start
  207.2 98.7 %all-reduce.9.cloned.1.call-start = ((), (), s32[]{:S(2)}) async-start(), calls=%async_computation.2 | async-start | bytes 4194304 | tf_op jit(solution)/shard_map/psum | solution.py:117
  208.4 20.1 %copy-start.4 = (f32[2,128,128]{2,1,0:T(8,128)S(1)}, f32[2,128,128]{2,1,0:T(8,128)}, u32[]{:S(2)}) copy-start(f32[2,128,128]{2,1,0:T(8,128)} %param.5) | copy-start | bytes 393220
  228.5 148.3 %all-gather.3.cloned.1.call-start = ((), (), s32[]{:S(2)}) async-start(), calls=%async_computation.4 | async-start | bytes 3244032 | tf_op jit(solution)/shard_map/all_gather | solution.py:85
  242.3 193.0 %all-reduce.11.cloned.1.call-start = ((), (), s32[]{:S(2)}) async-start(), calls=%async_computation.3 | async-start | bytes 2097152 | tf_op jit(solution)/shard_map/psum | solution.py:127
  242.3 65.3 %collective-permute-start.3 = (f32[4096,128]{1,0:T(8,128)}, f32[4096,128]{1,0:T(8,128)S(1)}, u32[]{:S(2)}, u32[]{:S(2)}) collective-permute-start(f32[4096,128]{1,0:T(8,128)} %collective-permute-done.2), channel_id=1, source_target_pairs={{0,1},{1,2},{2,3},{3,0},{4,5},{5,6},{6,7},{7,4},{8,9},{9,10},{10,1... | collective-permute-start | bytes 6291464 | tf_op jit(solution)/shard_map/ppermute | solution.py:53
  243.9 94.1 %collective-permute-start.4 = (f32[4096,128]{1,0:T(8,128)}, f32[4096,128]{1,0:T(8,128)}, u32[]{:S(2)}, u32[]{:S(2)}) collective-permute-start(f32[4096,128]{1,0:T(8,128)} %collective-permute-done.1), channel_id=1, source_target_pairs={{0,3},{1,0},{2,1},{3,2},{4,7},{5,4},{6,5},{7,6},{8,11},{9,8},{10,9... | collective-permute-start | bytes 6291464 | tf_op jit(solution)/shard_map/ppermute | solution.py:54
  390.0 7.5 %copy-start.1 = (f32[256,256]{0,1:T(8,128)S(1)}, f32[256,256]{0,1:T(8,128)}, u32[]{:S(2)}) copy-start(f32[256,256]{0,1:T(8,128)} %convolution_negate_fusion.1) | copy-start | bytes 786436
  393.3 6.2 %copy-start.2 = (f32[1,1,256,256]{2,3,1,0:T(8,128)S(1)}, f32[1,1,256,256]{2,3,1,0:T(8,128)}, u32[]{:S(2)}) copy-start(f32[1,1,256,256]{2,3,1,0:T(8,128)} %copy.36) | copy-start | bytes 786436
  435.3 3.2 copy-start.3
  435.3 3.3 copy-start.5
  435.3 3.3 copy-start.6
Sparse Core Ops, SparseCore 0:
  40.8 59.3 all-reduce.12
  207.3 33.4 reduce-scatter.1
  244.0 61.7 all-reduce.8
  308.5 68.2 all-gather.2
  379.8 55.4 all-reduce.10
where the time goes:
time: 495 us; the launch traced here: 486 us
  waiting for transfers between devices  265 us (54%)
  matrix products  126 us (25%)
  local copies, waits for them, and re-layouts  51.2 us (10%)
  between operations  17 us (3%)
  other arithmetic  14.1 us (3%)
  starting transfers between devices  13.3 us (3%)
    ppermute x3, waiting for transfers between devices, ring_gather(): lax.ppermute(upper[i], 'col', down)  74.6 us
    dot_general x6, matrix products, product_t(): lax.dot_general(left, right, (((0,), (0,)), ((), ())), precision=precisio...  71 us
    psum x1, waiting for transfers between devices, shards(): joined = lax.psum(after(joined, [summed[0], inner] + pairs), 'row')  59.5 us
    dot_general x11, matrix products, matmul(): jnp.dot(left, right, precision=precision, preferred_element_type=jnp.floa...  54.5 us
    psum x1, waiting for transfers between devices, shards(): lax.psum((product_t(basis[0], vectors), product_t(basis[0], basis[0], FUL...  54.5 us
    ppermute x2, waiting for transfers between devices, ring_gather(): lower = [lax.ppermute(lower[i], 'col', up) for i in range(count)]  32.8 us
    unnamed x31, local copies, waits for them, and re-layouts  25.4 us
    psum x1, waiting for transfers between devices, shards(): summed[last] = lax.psum(after(product_t(basis[last], vectors), done), 'row')  17 us
  transfers between devices with their start and end apart: 11, of which 8 were waited for; matrix products, arithmetic and copies ran while one was open for 27% of the time, Pallas kernels for 0%

commit v1 on v0

v1 whole, which is shorter than its diff:
```python
import functools

import jax
import jax.numpy as jnp
from jax import lax
from jax.experimental import pallas as pl
from jax.experimental.pallas import tpu as pltpu
from jax.sharding import PartitionSpec as P

F32, BF16 = jnp.float32, jnp.bfloat16
MESH = pl.DeviceIdType.MESH
VMEM_BYTES = 67043328
CHUNK = 256


def split(value):
    high = value.astype(BF16)
    return high, (value - high.astype(F32)).astype(BF16)


def dot(left, right):
    return jnp.dot(left, right, preferred_element_type=F32)


def exact(left, right):
    return jnp.dot(left, right, precision=lax.Precision.HIGHEST, preferred_element_type=F32)


class Line:
    def __init__(self, n, per_dev):
        self.n, self.per_dev = n, per_dev
        self.first = per_dev - per_dev // 2
        self.last = per_dev - self.first

    def below(self, z, q):
        return self.per_dev * z - 1 - q

    def above(self, z, q):
        n, first, last = self.n, self.first, self.last
        lead = (n - 1 - z) * first
        outward = self.per_dev * (z + 1 + q // first) + self.per_dev - 1 - q % first
        if not last:
            return outward
        rest = q - lead
        inward = self.per_dev * (n - 1 - rest // last) + last - 1 - rest % last
        if isinstance(z, int):
            return outward if q < lead else inward
        return jnp.where(q < lead, outward, inward)

    def needed(self, z, panel):
        owner = panel // self.per_dev
        if owner == z:
            return 0
        if owner < z:
            return 2 * (self.per_dev * z - panel)
        order = [self.above(z, q) for q in range(self.per_dev * (self.n - 1 - z))]
        return 2 * (order.index(panel) + 1)


def groups_of(panels):
    final = max(1, 3 * panels // 8)
    middle = min(panels - final, 3 * panels // 8)
    groups = []
    for low, high in ((final + middle, panels), (final, final + middle)):
        if high > low:
            order = [high - 1, *range(low, high - 1)]
            groups.append((order, order))
    groups.append(([*range(final - 2, -1, -1), final - 1], [*range(final - 1, -1, -1)]))
    return groups


def kernel(n, g, groups, x_in, v_in, t_in, x_out, v_out, y_out,
           X, V, T, acc, pair, half, parts, red, yb,
           local_sem, up_send, up_recv, dn_send, dn_recv, tz_send, tz_recv, tr_send, tr_recv,
           a_send, a_recv, b_send, b_recv, c_send, c_recv, d_send, d_recv):
    panels, rows, nb = V.shape
    per_dev = v_in.shape[0]
    cols = X.shape[1]
    unit = rows // 2
    line = Line(n, per_dev)
    chips = g // 2
    z, me = lax.axis_index("col"), lax.axis_index("row")
    core, chip = lax.rem(me, 2), lax.div(me, 2)
    partner = me + 1 - 2 * core
    quarter = nb // g

    barrier = pltpu.get_barrier_semaphore()
    for d in range(1, g):
        pl.semaphore_signal(barrier, inc=1, device_id={"row": lax.rem(me + d, g)}, device_id_type=MESH)
    for d in range(1, n):
        pl.semaphore_signal(barrier, inc=1, device_id={"col": lax.rem(z + d, n)}, device_id_type=MESH)
    pl.semaphore_wait(barrier, g - 1 + n - 1)

    def remote(src, dst, send, recv, where):
        return pltpu.make_async_remote_copy(
            src_ref=src, dst_ref=dst, send_sem=send, recv_sem=recv, device_id=where, device_id_type=MESH
        )

    def piece(panel, at):
        return V.at[panel, pl.ds(at * unit, unit)]

    def own(j, at):
        return v_in.at[j, pl.ds(at * unit, unit)]

    def up(k, src, dst):
        return remote(src, dst, up_send.at[k], up_recv.at[k], {"col": lax.rem(z + 1, n)})

    def down(k, src, dst):
        return remote(src, dst, dn_send.at[k], dn_recv.at[k], {"col": lax.rem(z + n - 1, n)})

    def send_last():
        for i in range(2 * line.last):
            j = line.last - 1 - i // 2
            down(2 * (line.first + per_dev * (n - 1 - z)) + i, own(j, i % 2), piece(per_dev * z + j, i % 2)).start()

    @pl.when(z < n - 1)
    def _():
        for k in range(2 * per_dev):
            j = per_dev - 1 - k // 2
            up(k, own(j, k % 2), piece(per_dev * z + j, k % 2)).start()

    @pl.when(z > 0)
    def _():
        for k in range(2 * line.first):
            j = per_dev - 1 - k // 2
            down(k, own(j, k % 2), piece(per_dev * z + j, k % 2)).start()

    @pl.when(z == n - 1)
    def _():
        send_last()

    mine = pl.ds(me * quarter, quarter)
    owned = pl.ds(z * per_dev, per_dev)
    t_own = pltpu.make_async_copy(t_in.at[:, mine], T.at[owned, mine], local_sem.at[0])
    t_own.start()
    t_across = [
        remote(t_in.at[:, mine], T.at[owned, mine], tz_send.at[d - 1], tz_recv.at[d - 1], {"col": lax.rem(z + d, n)})
        for d in range(1, n)
    ]
    for copy in t_across:
        copy.start()
    v_own = pltpu.make_async_copy(v_in, V.at[owned], local_sem.at[1])
    v_own.start()
    x_load = pltpu.make_async_copy(x_in, X, local_sem.at[2])
    x_load.start()
    t_own.wait()
    for copy in t_across:
        copy.wait()
    t_along = [
        remote(T.at[:, mine], T.at[:, mine], tr_send.at[d - 1], tr_recv.at[d - 1], {"row": lax.rem(me + d, g)})
        for d in range(1, g)
    ]
    for copy in t_along:
        copy.start()
    v_own.wait()
    x_load.wait()
    for copy in t_along:
        copy.wait()

    def service(u):
        q, at = u // 2, u % 2

        @pl.when(u < 2 * per_dev * z)
        def _():
            spot = piece(line.below(z, q), at)
            up(u, spot, spot).wait_recv()

            @pl.when(z < n - 1)
            def _():
                if u + 2 * per_dev < 2 * per_dev * (n - 1):
                    up(u + 2 * per_dev, spot, spot).start()

        @pl.when(u < 2 * per_dev * (n - 1 - z))
        def _():
            spot = piece(line.above(z, q), at)
            down(u, spot, spot).wait_recv()

            @pl.when(z > 0)
            def _():
                if u + 2 * line.first < 2 * per_dev * (n - 1):
                    down(u + 2 * line.first, spot, spot).start()

            if line.last:

                @pl.when((z > 0) & (u == 2 * per_dev * (n - 1 - z) - 1))
                def _():
                    send_last()

    served = [0]

    def ensure(count):
        for u in range(served[0], count):
            service(u)
        served[0] = max(served[0], count)

    def clear(s, width):
        acc[s, :, pl.ds(0, width)] = jnp.zeros((nb, width), F32)

    def product(s, panel, before, start, count):
        width = cols + nb * len(before)

        @pl.loop(0, count // CHUNK)
        def _(i):
            span = pl.ds(pl.multiple_of(start + i * CHUNK, CHUNK), CHUNK)
            high, low = split(V[panel, span, :].T)
            right = jnp.concatenate([X[span, :]] + [V[b, span, :] for b in before], axis=1)
            right_high, right_low = split(right)
            both = dot(jnp.concatenate([high, low], axis=0), right_high)
            acc[s, :, pl.ds(0, width)] += both[:nb] + both[nb:] + dot(high, right_low)

    top = nb // 2
    tall = top // chips

    def sum_a(s, width):
        cut = pl.ds(0, width)
        remote(acc.at[s, pl.ds(top * (1 - core), top), cut], pair.at[s, :, cut], a_send.at[s], a_recv.at[s], {"row": partner}).start()

    def sum_b(s, width):
        cut = pl.ds(0, width)
        kept = acc.at[s, pl.ds(top * core, top), cut]
        remote(kept, pair.at[s, :, cut], a_send.at[s], a_recv.at[s], {"row": partner}).wait()
        half[s, :, cut] = kept[...] + pair[s, :, cut]
        for d in range(1, chips):
            other = lax.rem(chip + d, chips)
            remote(
                half.at[s, pl.ds(other * tall, tall), cut], parts.at[s, d - 1, :, cut],
                b_send.at[s, d - 1], b_recv.at[s, d - 1], {"row": 2 * other + core},
            ).start()

    def sum_c(s, width):
        cut = pl.ds(0, width)
        here = half.at[s, pl.ds(chip * tall, tall), cut]
        total = here[...]
        for d in range(1, chips):
            other = lax.rem(chip + d, chips)
            remote(here, parts.at[s, d - 1, :, cut], b_send.at[s, d - 1], b_recv.at[s, d - 1], {"row": 2 * other + core}).wait()
            total = total + parts[s, d - 1, :, cut]
        spot = red.at[s, pl.ds(top * core + chip * tall, tall), cut]
        spot[...] = total
        for d in range(1, chips):
            other = lax.rem(chip + d, chips)
            remote(spot, spot, c_send.at[s, d - 1], c_recv.at[s, d - 1], {"row": 2 * other + core}).start()

    def sum_d(s, width):
        cut = pl.ds(0, width)
        for d in range(1, chips):
            source = lax.rem(chip + chips - d, chips)
            spot = red.at[s, pl.ds(top * core + source * tall, tall), cut]
            remote(spot, spot, c_send.at[s, d - 1], c_recv.at[s, d - 1], {"row": 2 * source + core}).wait()
        spot = red.at[s, pl.ds(top * core, top), cut]
        remote(spot, spot, d_send.at[s], d_recv.at[s], {"row": partner}).start()

    def sum_e(s, width):
        cut = pl.ds(0, width)
        spot = red.at[s, pl.ds(top * (1 - core), top), cut]
        remote(spot, spot, d_send.at[s], d_recv.at[s], {"row": partner}).wait()

    steps = [sum_a, sum_b, sum_c, sum_d, sum_e]

    def solve(base, order, low, store):
        solved = {}
        for panel in sorted(order, reverse=True):
            at = order.index(panel)
            value = red[base + at, :, pl.ds(0, cols)]
            for later in solved:
                behind = order.index(later)
                if at > behind:
                    gram = red[base + at, :, pl.ds(cols + nb * behind, nb)]
                else:
                    gram = red[base + behind, :, pl.ds(cols + nb * at, nb)].T
                value = value - exact(gram, solved[later])
            solved[panel] = exact(T[panel], value)
            store(panel - low, solved[panel])

    base = 0
    for index, (near, far) in enumerate(groups):
        count, low = len(near), min(near)
        size = nb * count
        if index == len(groups) - 1:
            save = pltpu.make_async_copy(X, x_out, local_sem.at[0])
            save.start()
        pending = []

        def advance():
            for item in pending:
                steps[item[2]](item[0], item[1])
                item[2] += 1
            pending[:] = [item for item in pending if item[2] < len(steps)]

        done = []
        for k in range(count):
            panel = near[k] if near[k] == far[k] else jnp.where(z < n // 2, near[k], far[k])
            wait = max(
                line.needed(place, near[k] if place < n // 2 else far[k]) for place in range(n)
            )
            width = cols + nb * k
            clear(base + k, width)
            if index == len(groups) - 1 and k == count - 1:
                ensure(wait - 1)
                product(base + k, panel, done, 0, unit)
                ensure(2 * per_dev * (n - 1))
                product(base + k, panel, done, unit, unit)
            else:
                ensure(wait)
                product(base + k, panel, done, 0, rows)
            if index == len(groups) - 1:
                pltpu.make_async_copy(V.at[panel], v_out.at[:, pl.ds(pl.multiple_of((panel - low) * nb, nb), nb)], local_sem.at[1 + k]).start()
            pending.append([base + k, width, 0])
            advance()
            done.append(panel)
        while pending:
            advance()

        if index < len(groups) - 1:

            def store(at, value):
                high, rest = split(value)
                yb[pl.ds(at * nb, nb), :] = high
                yb[pl.ds(size + at * nb, nb), :] = high
                yb[pl.ds(2 * size + at * nb, nb), :] = rest

            solve(base, near, low, store)

            @pl.loop(0, rows // CHUNK)
            def _(i):
                span = pl.ds(pl.multiple_of(i * CHUNK, CHUNK), CHUNK)
                high, rest = split(jnp.concatenate([V[low + p, span, :] for p in range(count)], axis=1))
                X[span, :] -= dot(jnp.concatenate([high, rest, high], axis=1), yb[pl.ds(0, 3 * size), :])
        else:

            def store(at, value):
                y_out[pl.ds(at * nb, nb), :] = value

            @pl.when(z < n // 2)
            def _():
                solve(base, near, low, store)

            @pl.when(z >= n // 2)
            def _():
                solve(base, far, low, store)

            save.wait()
            for k in range(count):
                panel = jnp.where(z < n // 2, near[k], far[k])
                pltpu.make_async_copy(V.at[panel], v_out.at[:, pl.ds(pl.multiple_of((panel - low) * nb, nb), nb)], local_sem.at[1 + k]).wait()
        base += count

    for k in range(2 * per_dev * (n - 1)):

        @pl.when((z < n - 1) & (k < 2 * per_dev * (z + 1)))
        def _():
            up(k, piece(0, 0), piece(0, 0)).wait_send()

        @pl.when((z > 0) & (k < 2 * per_dev * (n - z)))
        def _():
            down(k, piece(0, 0), piece(0, 0)).wait_send()


def shards(n, g, vectors, reflectors, triangles):
    per_dev, rows, nb = reflectors.shape
    cols = vectors.shape[1]
    panels = per_dev * n
    groups = groups_of(panels)
    most = max(len(near) for near, _ in groups)
    final = len(groups[-1][0])
    wide = cols + nb * (most - 1)
    chips = g // 2
    sems = pltpu.SemaphoreType.DMA
    anywhere = pl.BlockSpec(memory_space=pl.ANY)
    ends = 2 * per_dev * (n - 1)
    peers = max(1, chips - 1)
    early, basis, scaled = pl.pallas_call(
        functools.partial(kernel, n, g, groups),
        out_shape=(
            jax.ShapeDtypeStruct((rows, cols), F32),
            jax.ShapeDtypeStruct((rows, nb * final), F32),
            jax.ShapeDtypeStruct((nb * final, cols), F32),
        ),
        in_specs=[anywhere] * 3,
        out_specs=(anywhere, anywhere, pl.BlockSpec(memory_space=pltpu.VMEM)),
        scratch_shapes=[
            pltpu.VMEM((rows, cols), F32),
            pltpu.VMEM((panels, rows, nb), F32),
            pltpu.VMEM((panels, nb, nb), F32),
            pltpu.VMEM((panels, nb, wide), F32),
            pltpu.VMEM((panels, nb // 2, wide), F32),
            pltpu.VMEM((panels, nb // 2, wide), F32),
            pltpu.VMEM((panels, peers, nb // 2 // chips, wide), F32),
            pltpu.VMEM((panels, nb, wide), F32),
            pltpu.VMEM((3 * nb * most, cols), BF16),
            sems((max(3, 1 + final),)),
            sems((ends,)), sems((ends,)), sems((ends,)), sems((ends,)),
            sems((n - 1,)), sems((n - 1,)), sems((g - 1,)), sems((g - 1,)),
            sems((panels,)), sems((panels,)),
            sems((panels, peers)), sems((panels, peers)), sems((panels, peers)), sems((panels, peers)),
            sems((panels,)), sems((panels,)),
        ],
        compiler_params=pltpu.CompilerParams(
            collective_id=0, has_side_effects=True, vmem_limit_bytes=VMEM_BYTES
        ),
    )(vectors, reflectors, triangles)
    return early - jnp.dot(basis, scaled, precision=lax.Precision.HIGH, preferred_element_type=F32)


def solution(mesh):
    n, g = mesh.shape["col"], mesh.shape["row"]
    placed = (P("row", "col"), P("col", "row", None), P("col", None, None))
    return jax.shard_map(
        functools.partial(shards, n, g), mesh=mesh, in_specs=placed, out_specs=P("row", "col"), check_vma=False
    )
```

time: 495 us -> 415 us (0.84); the launches traced: 486 us -> 415 us
  Pallas kernels: 0 us -> 393 us
  waiting for transfers between devices: 265 us -> 0 us
  matrix products: 126 us -> 21.6 us
  local copies, waits for them, and re-layouts: 51.2 us -> 0 us
  between operations: 17 us -> 0.01 us
  other arithmetic: 14.1 us -> 0 us
  starting transfers between devices: 13.3 us -> 0 us
    pallas_call x0 -> x1, Pallas kernels: none -> 393 us  [shards(): pl.pallas_call(functools.partial(kernel, n, g, groups), out_shape=(jax.Sh...]
    psum x3 -> x0, waiting for transfers between devices: 131 us -> none  [the longest x1 59.5 us: shards(): joined = lax.psum(after(joined, [summed[0], inner] + pairs), 'row')]
    ppermute x6 -> x0, waiting for transfers between devices: 107 us -> none  [the longest x3 74.6 us: ring_gather(): lax.ppermute(upper[i], 'col', down)]
    dot_general x17 -> x1, matrix products: 126 us -> 21.6 us  [shards(): jnp.dot(basis, scaled, precision=lax.Precision.HIGH, preferred_element_ty...]
    unnamed x31 -> x0, local copies, waits for them, and re-layouts: 25.4 us -> none
    all_gather x1 -> x0, waiting for transfers between devices: 16.2 us -> none  [shards(): shared = lax.all_gather(jnp.stack(mine), ('col', 'row'), axis=0)]
    ppermute x6 -> x0, starting transfers between devices: 12.9 us -> none  [the longest x3 11.4 us: ring_gather(): lax.ppermute(upper[i], 'col', down)]
    reduce_scatter x1 -> x0, waiting for transfers between devices: 10.3 us -> none  [shards(): lax.psum_scatter(jnp.stack(pairs), 'row', scatter_dimension=1, tiled=True)]
  transfers between devices with their start and end apart: 11 -> 0, of which waited for: 8 -> 0; matrix products, arithmetic and copies ran while one was open for 27% -> 0% of each run, Pallas kernels for 0% -> 0%
where the time goes in v1:
time: 415 us
  Pallas kernels  393 us (95%)
  matrix products  21.6 us (5%)
    pallas_call x1, Pallas kernels, shards(): pl.pallas_call(functools.partial(kernel, n, g, groups), out_shape=(jax.Sh...  393 us
    dot_general x1, matrix products, shards(): jnp.dot(basis, scaled, precision=lax.Precision.HIGH, preferred_element_ty...  21.6 us

profile of v1, /device:TPU:0, one launch (start us, length us, event | category | flops | bytes accessed | tf_op | source)
XLA Modules:
  0.0 414.9 jit_solution(219333710981078509)
XLA Ops:
  0.0 393.3 %shard_map.37 = (f32[4096,1024]{1,0:T(8,128)}, f32[4096,384]{1,0:T(8,128)}, f32[384,1024]{1,0:T(8,128)}) custom-call(f32[4096,1024]{1,0:T(8,128)} %x_in.1, f32[2,4096,128]{2,1,0:T(8,128)} %v_in.1, f32[2,128,128]{2,1,0:T(8,128)} %t_in.1), custom_call_target="tpu_custom_call" | custom-call | tf_op jit(solution)/shard_map/pallas_call | solution.py:372
  393.3 21.6 %convolution_subtract_fusion = f32[4096,1024]{1,0:T(8,128)} fusion(f32[4096,1024]{1,0:T(8,128)} %get-tuple-element.8, f32[4096,384]{1,0:T(8,128)} %get-tuple-element.9, f32[384,1024]{1,0:T(8,128)} %get-tuple-element.10), kind=kOutput, calls=%fused_computation | convolution fusion | flops 9667870720 | bytes 41418752 | tf_op jit(solution)/shard_map/dot_general | solution.py:402

commit v2 on v1

--- a/solution.py
+++ b/solution.py
@@ -10,7 +10,9 @@
 F32, BF16 = jnp.float32, jnp.bfloat16
 MESH = pl.DeviceIdType.MESH
 VMEM_BYTES = 67043328
-CHUNK = 256
+CHUNK = 512
+STEP = 512
+LAST = 512
 
 
 def split(value):
@@ -23,7 +25,12 @@
 
 
 def exact(left, right):
-    return jnp.dot(left, right, precision=lax.Precision.HIGHEST, preferred_element_type=F32)
+    left_high, left_low = split(left)
+    right_high, right_low = split(right)
+    return dot(
+        jnp.concatenate([left_high, left_low, left_high], axis=1),
+        jnp.concatenate([right_high, right_high, right_low], axis=0),
+    )
 
 
 class Line:
@@ -57,20 +64,20 @@
         return 2 * (order.index(panel) + 1)
 
 
-def groups_of(panels):
-    final = max(1, 3 * panels // 8)
-    middle = min(panels - final, 3 * panels // 8)
-    groups = []
-    for low, high in ((final + middle, panels), (final, final + middle)):
-        if high > low:
-            order = [high - 1, *range(low, high - 1)]
-            groups.append((order, order))
-    groups.append(([*range(final - 2, -1, -1), final - 1], [*range(final - 1, -1, -1)]))
-    return groups
-
-
-def kernel(n, g, groups, x_in, v_in, t_in, x_out, v_out, y_out,
-           X, V, T, acc, pair, half, parts, red, yb,
+class Plan:
+    def __init__(self, panels):
+        self.final = max(1, 3 * panels // 8)
+        low = self.final
+        self.first = [low, low + 2, *range(panels - 1, low + 2, -1)]
+        self.chosen = [*range(low + 2, panels)]
+        self.near = [*range(low - 2, -1, -1), low - 1]
+        self.far = [*range(low - 1, -1, -1)]
+        self.grams = max(len(self.first) - 1, low)
+        self.update = max(len(self.chosen), low)
+
+
+def kernel(n, g, plan, x_in, v_in, t_in, x_out, v_out, y_out,
+           X, V, T, acc, pair, half, parts, red, yb, Y,
            local_sem, up_send, up_recv, dn_send, dn_recv, tz_send, tz_recv, tr_send, tr_recv,
            a_send, a_recv, b_send, b_recv, c_send, c_recv, d_send, d_recv):
     panels, rows, nb = V.shape
@@ -139,23 +146,12 @@
     ]
     for copy in t_across:
         copy.start()
-    v_own = pltpu.make_async_copy(v_in, V.at[owned], local_sem.at[1])
-    v_own.start()
-    x_load = pltpu.make_async_copy(x_in, X, local_sem.at[2])
-    x_load.start()
-    t_own.wait()
-    for copy in t_across:
-        copy.wait()
     t_along = [
         remote(T.at[:, mine], T.at[:, mine], tr_send.at[d - 1], tr_recv.at[d - 1], {"row": lax.rem(me + d, g)})
         for d in range(1, g)
     ]
-    for copy in t_along:
-        copy.start()
-    v_own.wait()
-    x_load.wait()
-    for copy in t_along:
-        copy.wait()
+    v_own = pltpu.make_async_copy(v_in, V.at[owned], local_sem.at[1])
+    x_load = pltpu.make_async_copy(x_in, X, local_sem.at[2])
 
     def service(u):
         q, at = u // 2, u % 2
@@ -190,14 +186,17 @@
 
     def ensure(count):
         for u in range(served[0], count):
-            service(u)
+            with jax.named_scope(f"hop{u}"):
+                service(u)
         served[0] = max(served[0], count)
 
-    def clear(s, width):
-        acc[s, :, pl.ds(0, width)] = jnp.zeros((nb, width), F32)
+    slots = acc.shape[0]
 
     def product(s, panel, before, start, count):
         width = cols + nb * len(before)
+        total = acc.at[s % slots, :, pl.ds(0, width)]
+        if start == 0:
+            total[...] = jnp.zeros((nb, width), F32)
 
         @pl.loop(0, count // CHUNK)
         def _(i):
@@ -206,18 +205,18 @@
             right = jnp.concatenate([X[span, :]] + [V[b, span, :] for b in before], axis=1)
             right_high, right_low = split(right)
             both = dot(jnp.concatenate([high, low], axis=0), right_high)
-            acc[s, :, pl.ds(0, width)] += both[:nb] + both[nb:] + dot(high, right_low)
+            total[...] += both[:nb] + both[nb:] + dot(high, right_low)
 
     top = nb // 2
     tall = top // chips
 
     def sum_a(s, width):
         cut = pl.ds(0, width)
-        remote(acc.at[s, pl.ds(top * (1 - core), top), cut], pair.at[s, :, cut], a_send.at[s], a_recv.at[s], {"row": partner}).start()
+        remote(acc.at[s % slots, pl.ds(top * (1 - core), top), cut], pair.at[s, :, cut], a_send.at[s], a_recv.at[s], {"row": partner}).start()
 
     def sum_b(s, width):
         cut = pl.ds(0, width)
-        kept = acc.at[s, pl.ds(top * core, top), cut]
+        kept = acc.at[s % slots, pl.ds(top * core, top), cut]
         remote(kept, pair.at[s, :, cut], a_send.at[s], a_recv.at[s], {"row": partner}).wait()
         half[s, :, cut] = kept[...] + pair[s, :, cut]
         for d in range(1, chips):
@@ -257,124 +256,231 @@
 
     steps = [sum_a, sum_b, sum_c, sum_d, sum_e]
 
-    def solve(base, order, low, store):
-        solved = {}
-        for panel in sorted(order, reverse=True):
-            at = order.index(panel)
-            value = red[base + at, :, pl.ds(0, cols)]
-            for later in solved:
-                behind = order.index(later)
-                if at > behind:
-                    gram = red[base + at, :, pl.ds(cols + nb * behind, nb)]
-                else:
-                    gram = red[base + behind, :, pl.ds(cols + nb * at, nb)].T
-                value = value - exact(gram, solved[later])
-            solved[panel] = exact(T[panel], value)
-            store(panel - low, solved[panel])
-
-    base = 0
-    for index, (near, far) in enumerate(groups):
-        count, low = len(near), min(near)
-        size = nb * count
-        if index == len(groups) - 1:
-            save = pltpu.make_async_copy(X, x_out, local_sem.at[0])
-            save.start()
-        pending = []
-
-        def advance():
-            for item in pending:
-                steps[item[2]](item[0], item[1])
+    pending = []
+
+    def step(s):
+        for item in pending:
+            if item[0] == s:
+                with jax.named_scope(f"sum{s}_{item[2]}"):
+                    steps[item[2]](s, item[1])
                 item[2] += 1
-            pending[:] = [item for item in pending if item[2] < len(steps)]
-
-        done = []
-        for k in range(count):
-            panel = near[k] if near[k] == far[k] else jnp.where(z < n // 2, near[k], far[k])
-            wait = max(
-                line.needed(place, near[k] if place < n // 2 else far[k]) for place in range(n)
-            )
-            width = cols + nb * k
-            clear(base + k, width)
-            if index == len(groups) - 1 and k == count - 1:
-                ensure(wait - 1)
-                product(base + k, panel, done, 0, unit)
-                ensure(2 * per_dev * (n - 1))
-                product(base + k, panel, done, unit, unit)
-            else:
-                ensure(wait)
-                product(base + k, panel, done, 0, rows)
-            if index == len(groups) - 1:
-                pltpu.make_async_copy(V.at[panel], v_out.at[:, pl.ds(pl.multiple_of((panel - low) * nb, nb), nb)], local_sem.at[1 + k]).start()
-            pending.append([base + k, width, 0])
-            advance()
-            done.append(panel)
+        pending[:] = [item for item in pending if item[2] < len(steps)]
+
+    def advance():
+        for item in list(pending):
+            step(item[0])
+
+    def drain():
         while pending:
             advance()
 
-        if index < len(groups) - 1:
-
-            def store(at, value):
-                high, rest = split(value)
-                yb[pl.ds(at * nb, nb), :] = high
-                yb[pl.ds(size + at * nb, nb), :] = high
-                yb[pl.ds(2 * size + at * nb, nb), :] = rest
-
-            solve(base, near, low, store)
-
-            @pl.loop(0, rows // CHUNK)
-            def _(i):
-                span = pl.ds(pl.multiple_of(i * CHUNK, CHUNK), CHUNK)
-                high, rest = split(jnp.concatenate([V[low + p, span, :] for p in range(count)], axis=1))
-                X[span, :] -= dot(jnp.concatenate([high, rest, high], axis=1), yb[pl.ds(0, 3 * size), :])
-        else:
-
-            def store(at, value):
-                y_out[pl.ds(at * nb, nb), :] = value
-
-            @pl.when(z < n // 2)
+    where, places = {}, {}
+
+    def form(name, before, wait, wait_half, between):
+        s, panel, behind = len(where), index_of(name), [index_of(b) for b in before]
+        with jax.named_scope(f"wait{s}"):
+            ensure(wait_half)
+        with jax.named_scope(f"product{s}"):
+            product(s, panel, behind, 0, unit)
+        between()
+        with jax.named_scope(f"wait{s}"):
+            ensure(wait)
+        with jax.named_scope(f"product{s}"):
+            product(s, panel, behind, unit, unit)
+        pending.append([s, cols + nb * len(before), 0])
+        step(s)
+        where[name] = s
+        places.update({(name, b): (s, at) for at, b in enumerate(before)})
+
+    def index_of(name):
+        if not isinstance(name, tuple):
+            return name
+        near, far = plan.near[name[0]], plan.far[name[0]]
+        return near if near == far else jnp.where(z < n // 2, near, far)
+
+    def units_for(name):
+        if not isinstance(name, tuple):
+            return max(line.needed(place, name) for place in range(n))
+        return max(
+            line.needed(place, (plan.near if place < n // 2 else plan.far)[name[0]]) for place in range(n)
+        )
+
+    def add(name, before, between):
+        wait = units_for(name)
+        form(name, before, wait, wait, between)
+
+    def gram(a, b):
+        if (a, b) in places:
+            s, at = places[a, b]
+            return red[s, :, pl.ds(cols + nb * at, nb)]
+        s, at = places[b, a]
+        return red[s, :, pl.ds(cols + nb * at, nb)].T
+
+    def solve(chosen, known, store, names=None):
+        names = names or {panel: panel for panel in chosen}
+        solved = dict(known)
+        for panel in sorted(chosen, reverse=True):
+            name = names[panel]
+            value = red[where[name], :, pl.ds(0, cols)]
+            for later in sorted(solved, reverse=True):
+                behind = names.get(later, later)
+                if (name, behind) in places or (behind, name) in places:
+                    value = value - exact(gram(name, behind), solved[later])
+            solved[panel] = exact(T[panel], value)
+            store(panel, solved[panel])
+
+    def keep(target, low, size):
+        def store(panel, value):
+            high, rest = split(value)
+            at = (panel - low) * nb
+            target[pl.ds(at, nb), :] = high
+            target[pl.ds(size + at, nb), :] = high
+            target[pl.ds(2 * size + at, nb), :] = rest
+
+        return store
+
+    ensure(1)
+    v_own.start()
+    x_load.start()
+    ensure(2 * per_dev)
+    t_own.wait()
+    for copy in t_across:
+        copy.wait()
+    for copy in t_along:
+        copy.start()
+    v_own.wait()
+    x_load.wait()
+
+    def update(low, count):
+        size = nb * count
+
+        @pl.loop(0, rows // STEP)
+        def _(i):
+            span = pl.ds(pl.multiple_of(i * STEP, STEP), STEP)
+            high, rest = split(jnp.concatenate([V[low + p, span, :] for p in range(count)], axis=1))
+            X[span, :] -= dot(jnp.concatenate([high, rest, high], axis=1), yb[pl.ds(0, 3 * size), :])
+
+    low = plan.final
+    last = plan.final - 1
+    lent = [low, low + 1]
+
+    def settle(chosen, known):
+        put = keep(yb, min(chosen), nb * len(chosen))
+
+        def store(panel, value):
+            put(panel, value)
+            Y[panel - low] = value
+
+        with jax.named_scope(f"solve{min(chosen)}"):
+            solve(chosen, {panel: Y[panel - low] for panel in known}, store)
+
+    for k, panel in enumerate(plan.first):
+        add(panel, plan.first[:k], advance)
+    drain()
+    for copy in t_along:
+        copy.wait()
+    settle(plan.chosen, [])
+    with jax.named_scope("update_chosen"):
+        update(low + 2, len(plan.chosen))
+
+    early = [(k,) for k in range(last)]
+    formed = [low]
+    for name in [*early[:1], low + 1, *early[1:]]:
+        add(name, formed, lambda: step(len(where) - 1))
+        formed = [*formed, name]
+    behind = [where[name] for name in early]
+
+    def nudge():
+        for s in behind:
+            step(s)
+
+    step(where[low + 1])
+    nudge()
+    while any(item[0] == where[low + 1] for item in pending):
+        step(where[low + 1])
+    settle(lent, plan.chosen)
+    nudge()
+    with jax.named_scope("update_lent"):
+        update(low, 2)
+    nudge()
+
+    save = pltpu.make_async_copy(X, x_out, local_sem.at[0])
+    save.start()
+    def give(panel, k):
+        spot = v_out.at[:, pl.ds(pl.multiple_of(panel * nb, nb), nb)]
+        return pltpu.make_async_copy(V.at[panel], spot, local_sem.at[1 + k])
+
+    ends = 2 * per_dev * (n - 1)
+
+    def prepare():
+        drain()
+        with jax.named_scope("prepare"):
+            for name in early:
+                spot = red.at[where[name], :, pl.ds(0, cols)]
+                value = spot[...]
+                for panel in lent:
+                    value = value - exact(gram(name, panel), Y[panel - low])
+                spot[...] = value
+        for k in range(ends - 2):
+
+            @pl.when((z < n - 1) & (k < 2 * per_dev * (z + 1) - 2))
             def _():
-                solve(base, near, low, store)
-
-            @pl.when(z >= n // 2)
+                up(k, piece(0, 0), piece(0, 0)).wait_send()
+
+            @pl.when((z > 0) & (k < 2 * per_dev * (n - z) - 2))
             def _():
-                solve(base, far, low, store)
-
-            save.wait()
-            for k in range(count):
-                panel = jnp.where(z < n // 2, near[k], far[k])
-                pltpu.make_async_copy(V.at[panel], v_out.at[:, pl.ds(pl.multiple_of((panel - low) * nb, nb), nb)], local_sem.at[1 + k]).wait()
-        base += count
-
-    for k in range(2 * per_dev * (n - 1)):
-
-        @pl.when((z < n - 1) & (k < 2 * per_dev * (z + 1)))
+                down(k, piece(0, 0), piece(0, 0)).wait_send()
+
+    for k in range(last):
+        give(index_of((k,)), k).start()
+    form((last,), early, ends, ends - 1, prepare)
+    give(index_of((last,)), last).start()
+    drain()
+    for order, here in ((plan.near, z < n // 2), (plan.far, z >= n // 2)):
+
+        @pl.when(here)
+        def _(order=order):
+            with jax.named_scope("solve_last"):
+                solve(order, {}, keep(y_out, 0, nb * plan.final), {panel: (k,) for k, panel in enumerate(order)})
+
+    save.wait()
+    for k in range(plan.final):
+        give(index_of((k,)), k).wait()
+
+    for k in range(2):
+
+        @pl.when(z < n - 1)
         def _():
-            up(k, piece(0, 0), piece(0, 0)).wait_send()
-
-        @pl.when((z > 0) & (k < 2 * per_dev * (n - z)))
+            up(2 * per_dev * (z + 1) - 2 + k, piece(0, 0), piece(0, 0)).wait_send()
+
+        @pl.when(z > 0)
         def _():
-            down(k, piece(0, 0), piece(0, 0)).wait_send()
+            down(2 * per_dev * (n - z) - 2 + k, piece(0, 0), piece(0, 0)).wait_send()
+
+
+def subtract(x, v, y, out):
+    high, rest = split(v[...])
+    out[...] = x[...] - dot(jnp.concatenate([high, rest, high], axis=1), y[...])
 
 
 def shards(n, g, vectors, reflectors, triangles):
     per_dev, rows, nb = reflectors.shape
     cols = vectors.shape[1]
     panels = per_dev * n
-    groups = groups_of(panels)
-    most = max(len(near) for near, _ in groups)
-    final = len(groups[-1][0])
-    wide = cols + nb * (most - 1)
+    plan = Plan(panels)
+    final = plan.final
+    wide = cols + nb * plan.grams
     chips = g // 2
     sems = pltpu.SemaphoreType.DMA
     anywhere = pl.BlockSpec(memory_space=pl.ANY)
     ends = 2 * per_dev * (n - 1)
     peers = max(1, chips - 1)
     early, basis, scaled = pl.pallas_call(
-        functools.partial(kernel, n, g, groups),
+        functools.partial(kernel, n, g, plan),
         out_shape=(
             jax.ShapeDtypeStruct((rows, cols), F32),
             jax.ShapeDtypeStruct((rows, nb * final), F32),
-            jax.ShapeDtypeStruct((nb * final, cols), F32),
+            jax.ShapeDtypeStruct((3 * nb * final, cols), BF16),
         ),
         in_specs=[anywhere] * 3,
         out_specs=(anywhere, anywhere, pl.BlockSpec(memory_space=pltpu.VMEM)),
@@ -382,12 +488,13 @@
             pltpu.VMEM((rows, cols), F32),
             pltpu.VMEM((panels, rows, nb), F32),
             pltpu.VMEM((panels, nb, nb), F32),
-            pltpu.VMEM((panels, nb, wide), F32),
+            pltpu.VMEM((3, nb, wide), F32),
             pltpu.VMEM((panels, nb // 2, wide), F32),
             pltpu.VMEM((panels, nb // 2, wide), F32),
             pltpu.VMEM((panels, peers, nb // 2 // chips, wide), F32),
             pltpu.VMEM((panels, nb, wide), F32),
-            pltpu.VMEM((3 * nb * most, cols), BF16),
+            pltpu.VMEM((3 * nb * plan.update, cols), BF16),
+            pltpu.VMEM((panels - final, nb, cols), F32),
             sems((max(3, 1 + final),)),
             sems((ends,)), sems((ends,)), sems((ends,)), sems((ends,)),
             sems((n - 1,)), sems((n - 1,)), sems((g - 1,)), sems((g - 1,)),
@@ -399,7 +506,17 @@
             collective_id=0, has_side_effects=True, vmem_limit_bytes=VMEM_BYTES
         ),
     )(vectors, reflectors, triangles)
-    return early - jnp.dot(basis, scaled, precision=lax.Precision.HIGH, preferred_element_type=F32)
+    return pl.pallas_call(
+        subtract,
+        grid=(rows // LAST,),
+        out_shape=jax.ShapeDtypeStruct((rows, cols), F32),
+        in_specs=[
+            pl.BlockSpec((LAST, cols), lambda i: (i, 0)),
+            pl.BlockSpec((LAST, nb * final), lambda i: (i, 0)),
+            pl.BlockSpec((3 * nb * final, cols), lambda i: (0, 0)),
+        ],
+        out_specs=pl.BlockSpec((LAST, cols), lambda i: (i, 0)),
+    )(early, basis, scaled)
 
 
 def solution(mesh):

time: 415 us -> 319 us (0.77)
  Pallas kernels: 393 us -> 319 us
  matrix products: 21.6 us -> 0 us
    pallas_call x1 -> x2, Pallas kernels: 393 us -> 319 us  [the longest x1 299 us: shards(): pl.pallas_call(functools.partial(kernel, n, g, plan), out_shape=(jax.Shap...]
    dot_general x1 -> x0, matrix products: 21.6 us -> none  [shards(): jnp.dot(basis, scaled, precision=lax.Precision.HIGH, preferred_element_ty...]
where the time goes in v2:
time: 319 us
  Pallas kernels  319 us (100%)
    pallas_call x1, Pallas kernels, shards(): pl.pallas_call(functools.partial(kernel, n, g, plan), out_shape=(jax.Shap...  299 us
    pallas_call x1, Pallas kernels, shards(): pl.pallas_call(subtract, grid=(rows // LAST,), out_shape=jax.ShapeDtypeSt...  19.8 us

profile of v2, /device:TPU:0, one launch (start us, length us, event | category | flops | bytes accessed | tf_op | source)
XLA Modules:
  0.0 319.1 jit_solution(5103647465025143998)
XLA Ops:
  0.0 299.3 %shard_map.37 = (f32[4096,1024]{1,0:T(8,128)}, f32[4096,384]{1,0:T(8,128)}, bf16[1152,1024]{1,0:T(8,128)(2,1)}) custom-call(f32[4096,1024]{1,0:T(8,128)} %x_in.1, f32[2,4096,128]{2,1,0:T(8,128)} %v_in.1, f32[2,128,128]{2,1,0:T(8,128)} %t_in.1), custom_call_target="tpu_custom_call" | custom-call | tf_op jit(solution)/shard_map/pallas_call | solution.py:478
  299.3 19.8 %shard_map.38 = f32[4096,1024]{1,0:T(8,128)} custom-call(f32[4096,1024]{1,0:T(8,128)} %get-tuple-element.8.x, f32[4096,384]{1,0:T(8,128)} %get-tuple-element.9.v, bf16[1152,1024]{1,0:T(8,128)(2,1)} %get-tuple-element.10.y), custom_call_target="tpu_custom_call" | custom-call | tf_op jit(solution)/shard_map/pallas_call | solution.py:509

commit v3 on v2

--- a/solution.py
+++ b/solution.py
@@ -12,7 +12,8 @@
 VMEM_BYTES = 67043328
 CHUNK = 512
 STEP = 512
-LAST = 512
+PIECES = 4
+PARTS = 8
 
 
 def split(value):
@@ -59,9 +60,9 @@
         if owner == z:
             return 0
         if owner < z:
-            return 2 * (self.per_dev * z - panel)
+            return PIECES * (self.per_dev * z - panel)
         order = [self.above(z, q) for q in range(self.per_dev * (self.n - 1 - z))]
-        return 2 * (order.index(panel) + 1)
+        return PIECES * (order.index(panel) + 1)
 
 
 class Plan:
@@ -83,7 +84,7 @@
     panels, rows, nb = V.shape
     per_dev = v_in.shape[0]
     cols = X.shape[1]
-    unit = rows // 2
+    unit = rows // PIECES
     line = Line(n, per_dev)
     chips = g // 2
     z, me = lax.axis_index("col"), lax.axis_index("row")
@@ -116,21 +117,21 @@
         return remote(src, dst, dn_send.at[k], dn_recv.at[k], {"col": lax.rem(z + n - 1, n)})
 
     def send_last():
-        for i in range(2 * line.last):
-            j = line.last - 1 - i // 2
-            down(2 * (line.first + per_dev * (n - 1 - z)) + i, own(j, i % 2), piece(per_dev * z + j, i % 2)).start()
+        for i in range(PIECES * line.last):
+            j = line.last - 1 - i // PIECES
+            down(PIECES * (line.first + per_dev * (n - 1 - z)) + i, own(j, i % PIECES), piece(per_dev * z + j, i % PIECES)).start()
 
     @pl.when(z < n - 1)
     def _():
-        for k in range(2 * per_dev):
-            j = per_dev - 1 - k // 2
-            up(k, own(j, k % 2), piece(per_dev * z + j, k % 2)).start()
+        for k in range(PIECES * per_dev):
+            j = per_dev - 1 - k // PIECES
+            up(k, own(j, k % PIECES), piece(per_dev * z + j, k % PIECES)).start()
 
     @pl.when(z > 0)
     def _():
-        for k in range(2 * line.first):
-            j = per_dev - 1 - k // 2
-            down(k, own(j, k % 2), piece(per_dev * z + j, k % 2)).start()
+        for k in range(PIECES * line.first):
+            j = per_dev - 1 - k // PIECES
+            down(k, own(j, k % PIECES), piece(per_dev * z + j, k % PIECES)).start()
 
     @pl.when(z == n - 1)
     def _():
@@ -154,31 +155,31 @@
     x_load = pltpu.make_async_copy(x_in, X, local_sem.at[2])
 
     def service(u):
-        q, at = u // 2, u % 2
-
-        @pl.when(u < 2 * per_dev * z)
+        q, at = u // PIECES, u % PIECES
+
+        @pl.when(u < PIECES * per_dev * z)
         def _():
             spot = piece(line.below(z, q), at)
             up(u, spot, spot).wait_recv()
 
             @pl.when(z < n - 1)
             def _():
-                if u + 2 * per_dev < 2 * per_dev * (n - 1):
-                    up(u + 2 * per_dev, spot, spot).start()
-
-        @pl.when(u < 2 * per_dev * (n - 1 - z))
+                if u + PIECES * per_dev < PIECES * per_dev * (n - 1):
+                    up(u + PIECES * per_dev, spot, spot).start()
+
+        @pl.when(u < PIECES * per_dev * (n - 1 - z))
         def _():
             spot = piece(line.above(z, q), at)
             down(u, spot, spot).wait_recv()
 
             @pl.when(z > 0)
             def _():
-                if u + 2 * line.first < 2 * per_dev * (n - 1):
-                    down(u + 2 * line.first, spot, spot).start()
+                if u + PIECES * line.first < PIECES * per_dev * (n - 1):
+                    down(u + PIECES * line.first, spot, spot).start()
 
             if line.last:
 
-                @pl.when((z > 0) & (u == 2 * per_dev * (n - 1 - z) - 1))
+                @pl.when((z > 0) & (u == PIECES * per_dev * (n - 1 - z) - 1))
                 def _():
                     send_last()
 
@@ -210,49 +211,49 @@
     top = nb // 2
     tall = top // chips
 
-    def sum_a(s, width):
-        cut = pl.ds(0, width)
-        remote(acc.at[s % slots, pl.ds(top * (1 - core), top), cut], pair.at[s, :, cut], a_send.at[s], a_recv.at[s], {"row": partner}).start()
-
-    def sum_b(s, width):
-        cut = pl.ds(0, width)
+    def sum_a(s, start, width, m):
+        cut = pl.ds(start, width)
+        remote(acc.at[s % slots, pl.ds(top * (1 - core), top), cut], pair.at[s, :, cut], a_send.at[m], a_recv.at[m], {"row": partner}).start()
+
+    def sum_b(s, start, width, m):
+        cut = pl.ds(start, width)
         kept = acc.at[s % slots, pl.ds(top * core, top), cut]
-        remote(kept, pair.at[s, :, cut], a_send.at[s], a_recv.at[s], {"row": partner}).wait()
+        remote(kept, pair.at[s, :, cut], a_send.at[m], a_recv.at[m], {"row": partner}).wait()
         half[s, :, cut] = kept[...] + pair[s, :, cut]
         for d in range(1, chips):
             other = lax.rem(chip + d, chips)
             remote(
                 half.at[s, pl.ds(other * tall, tall), cut], parts.at[s, d - 1, :, cut],
-                b_send.at[s, d - 1], b_recv.at[s, d - 1], {"row": 2 * other + core},
+                b_send.at[m, d - 1], b_recv.at[m, d - 1], {"row": 2 * other + core},
             ).start()
 
-    def sum_c(s, width):
-        cut = pl.ds(0, width)
+    def sum_c(s, start, width, m):
+        cut = pl.ds(start, width)
         here = half.at[s, pl.ds(chip * tall, tall), cut]
         total = here[...]
         for d in range(1, chips):
             other = lax.rem(chip + d, chips)
-            remote(here, parts.at[s, d - 1, :, cut], b_send.at[s, d - 1], b_recv.at[s, d - 1], {"row": 2 * other + core}).wait()
+            remote(here, parts.at[s, d - 1, :, cut], b_send.at[m, d - 1], b_recv.at[m, d - 1], {"row": 2 * other + core}).wait()
             total = total + parts[s, d - 1, :, cut]
         spot = red.at[s, pl.ds(top * core + chip * tall, tall), cut]
         spot[...] = total
         for d in range(1, chips):
             other = lax.rem(chip + d, chips)
-            remote(spot, spot, c_send.at[s, d - 1], c_recv.at[s, d - 1], {"row": 2 * other + core}).start()
-
-    def sum_d(s, width):
-        cut = pl.ds(0, width)
+            remote(spot, spot, c_send.at[m, d - 1], c_recv.at[m, d - 1], {"row": 2 * other + core}).start()
+
+    def sum_d(s, start, width, m):
+        cut = pl.ds(start, width)
         for d in range(1, chips):
             source = lax.rem(chip + chips - d, chips)
             spot = red.at[s, pl.ds(top * core + source * tall, tall), cut]
-            remote(spot, spot, c_send.at[s, d - 1], c_recv.at[s, d - 1], {"row": 2 * source + core}).wait()
+            remote(spot, spot, c_send.at[m, d - 1], c_recv.at[m, d - 1], {"row": 2 * source + core}).wait()
         spot = red.at[s, pl.ds(top * core, top), cut]
-        remote(spot, spot, d_send.at[s], d_recv.at[s], {"row": partner}).start()
-
-    def sum_e(s, width):
-        cut = pl.ds(0, width)
+        remote(spot, spot, d_send.at[m], d_recv.at[m], {"row": partner}).start()
+
+    def sum_e(s, start, width, m):
+        cut = pl.ds(start, width)
         spot = red.at[s, pl.ds(top * (1 - core), top), cut]
-        remote(spot, spot, d_send.at[s], d_recv.at[s], {"row": partner}).wait()
+        remote(spot, spot, d_send.at[m], d_recv.at[m], {"row": partner}).wait()
 
     steps = [sum_a, sum_b, sum_c, sum_d, sum_e]
 
@@ -261,14 +262,14 @@
     def step(s):
         for item in pending:
             if item[0] == s:
-                with jax.named_scope(f"sum{s}_{item[2]}"):
-                    steps[item[2]](s, item[1])
-                item[2] += 1
-        pending[:] = [item for item in pending if item[2] < len(steps)]
+                with jax.named_scope(f"sum{s}_{item[4]}"):
+                    steps[item[4]](*item[:4])
+                item[4] += 1
+        pending[:] = [item for item in pending if item[4] < len(steps)]
 
     def advance():
-        for item in list(pending):
-            step(item[0])
+        for s in dict.fromkeys(item[0] for item in pending):
+            step(s)
 
     def drain():
         while pending:
@@ -276,18 +277,22 @@
 
     where, places = {}, {}
 
-    def form(name, before, wait, wait_half, between):
+    def form(name, before, wait, wait_half, between, lead=rows // 2, halve=False):
         s, panel, behind = len(where), index_of(name), [index_of(b) for b in before]
         with jax.named_scope(f"wait{s}"):
             ensure(wait_half)
         with jax.named_scope(f"product{s}"):
-            product(s, panel, behind, 0, unit)
+            product(s, panel, behind, 0, lead)
         between()
         with jax.named_scope(f"wait{s}"):
             ensure(wait)
         with jax.named_scope(f"product{s}"):
-            product(s, panel, behind, unit, unit)
-        pending.append([s, cols + nb * len(before), 0])
+            product(s, panel, behind, lead, rows - lead)
+        width = cols + nb * len(before)
+        part = width // nb // 2 * nb if halve else width
+        pending.append([s, 0, part, s, 0])
+        if halve:
+            pending.append([s, part, width - part, panels, 0])
         step(s)
         where[name] = s
         places.update({(name, b): (s, at) for at, b in enumerate(before)})
@@ -329,20 +334,20 @@
             solved[panel] = exact(T[panel], value)
             store(panel, solved[panel])
 
-    def keep(target, low, size):
+    def keep(target, low, size, spots=(0, 1, 2)):
         def store(panel, value):
             high, rest = split(value)
             at = (panel - low) * nb
-            target[pl.ds(at, nb), :] = high
-            target[pl.ds(size + at, nb), :] = high
-            target[pl.ds(2 * size + at, nb), :] = rest
+            for k in spots[:-1]:
+                target[pl.ds(k * size + at, nb), :] = high
+            target[pl.ds(spots[-1] * size + at, nb), :] = rest
 
         return store
 
     ensure(1)
     v_own.start()
     x_load.start()
-    ensure(2 * per_dev)
+    ensure(PIECES * per_dev)
     t_own.wait()
     for copy in t_across:
         copy.wait()
@@ -410,7 +415,7 @@
         spot = v_out.at[:, pl.ds(pl.multiple_of(panel * nb, nb), nb)]
         return pltpu.make_async_copy(V.at[panel], spot, local_sem.at[1 + k])
 
-    ends = 2 * per_dev * (n - 1)
+    ends = PIECES * per_dev * (n - 1)
 
     def prepare():
         drain()
@@ -423,17 +428,17 @@
                 spot[...] = value
         for k in range(ends - 2):
 
-            @pl.when((z < n - 1) & (k < 2 * per_dev * (z + 1) - 2))
+            @pl.when((z < n - 1) & (k < PIECES * per_dev * (z + 1) - 2))
             def _():
                 up(k, piece(0, 0), piece(0, 0)).wait_send()
 
-            @pl.when((z > 0) & (k < 2 * per_dev * (n - z) - 2))
+            @pl.when((z > 0) & (k < PIECES * per_dev * (n - z) - 2))
             def _():
                 down(k, piece(0, 0), piece(0, 0)).wait_send()
 
     for k in range(last):
         give(index_of((k,)), k).start()
-    form((last,), early, ends, ends - 1, prepare)
+    form((last,), early, ends, ends - 1, prepare, rows - unit, True)
     give(index_of((last,)), last).start()
     drain()
     for order, here in ((plan.near, z < n // 2), (plan.far, z >= n // 2)):
@@ -441,7 +446,7 @@
         @pl.when(here)
         def _(order=order):
             with jax.named_scope("solve_last"):
-                solve(order, {}, keep(y_out, 0, nb * plan.final), {panel: (k,) for k, panel in enumerate(order)})
+                solve(order, {}, keep(y_out, 0, nb * plan.final, (0, 1)), {panel: (k,) for k, panel in enumerate(order)})
 
     save.wait()
     for k in range(plan.final):
@@ -451,16 +456,48 @@
 
         @pl.when(z < n - 1)
         def _():
-            up(2 * per_dev * (z + 1) - 2 + k, piece(0, 0), piece(0, 0)).wait_send()
+            up(PIECES * per_dev * (z + 1) - 2 + k, piece(0, 0), piece(0, 0)).wait_send()
 
         @pl.when(z > 0)
         def _():
-            down(2 * per_dev * (n - z) - 2 + k, piece(0, 0), piece(0, 0)).wait_send()
-
-
-def subtract(x, v, y, out):
-    high, rest = split(v[...])
-    out[...] = x[...] - dot(jnp.concatenate([high, rest, high], axis=1), y[...])
+            down(PIECES * per_dev * (n - z) - 2 + k, piece(0, 0), piece(0, 0)).wait_send()
+
+
+def subtract(sizes, x_in, v_in, y_in, out, X, V, Y, x_sem, v_sem, y_sem, out_sem):
+    depth = V.shape[1]
+    y_load = pltpu.make_async_copy(y_in, Y, y_sem)
+    y_load.start()
+
+    def span(i):
+        return pl.ds(sum(sizes[:i]), sizes[i])
+
+    def load(i):
+        return (
+            pltpu.make_async_copy(x_in.at[span(i)], X.at[span(i)], x_sem.at[i]),
+            pltpu.make_async_copy(v_in.at[span(i)], V.at[span(i)], v_sem.at[i]),
+        )
+
+    def save(i):
+        return pltpu.make_async_copy(X.at[span(i)], out.at[span(i)], out_sem.at[i])
+
+    ahead = 2
+    for i in range(ahead):
+        for copy in load(i):
+            copy.start()
+    y_load.wait()
+    for i in range(len(sizes)):
+        for copy in load(i):
+            copy.wait()
+        if i + ahead < len(sizes):
+            for copy in load(i + ahead):
+                copy.start()
+        high, rest = split(V[span(i)])
+        left = jnp.concatenate([high, rest, high], axis=1)
+        right = jnp.concatenate([Y[:depth], Y[:depth], Y[depth:]], axis=0)
+        X[span(i)] = X[span(i)] - dot(left, right)
+        save(i).start()
+    for i in range(len(sizes)):
+        save(i).wait()
 
 
 def shards(n, g, vectors, reflectors, triangles):
@@ -473,14 +510,14 @@
     chips = g // 2
     sems = pltpu.SemaphoreType.DMA
     anywhere = pl.BlockSpec(memory_space=pl.ANY)
-    ends = 2 * per_dev * (n - 1)
+    ends, sums = PIECES * per_dev * (n - 1), panels + 1
     peers = max(1, chips - 1)
     early, basis, scaled = pl.pallas_call(
         functools.partial(kernel, n, g, plan),
         out_shape=(
             jax.ShapeDtypeStruct((rows, cols), F32),
             jax.ShapeDtypeStruct((rows, nb * final), F32),
-            jax.ShapeDtypeStruct((3 * nb * final, cols), BF16),
+            jax.ShapeDtypeStruct((2 * nb * final, cols), BF16),
         ),
         in_specs=[anywhere] * 3,
         out_specs=(anywhere, anywhere, pl.BlockSpec(memory_space=pltpu.VMEM)),
@@ -498,24 +535,28 @@
             sems((max(3, 1 + final),)),
             sems((ends,)), sems((ends,)), sems((ends,)), sems((ends,)),
             sems((n - 1,)), sems((n - 1,)), sems((g - 1,)), sems((g - 1,)),
-            sems((panels,)), sems((panels,)),
-            sems((panels, peers)), sems((panels, peers)), sems((panels, peers)), sems((panels, peers)),
-            sems((panels,)), sems((panels,)),
+            sems((sums,)), sems((sums,)),
+            sems((sums, peers)), sems((sums, peers)), sems((sums, peers)), sems((sums, peers)),
+            sems((sums,)), sems((sums,)),
         ],
         compiler_params=pltpu.CompilerParams(
             collective_id=0, has_side_effects=True, vmem_limit_bytes=VMEM_BYTES
         ),
     )(vectors, reflectors, triangles)
+    size = rows // PARTS
+    sizes = [size // 2, *[size] * (PARTS - 1), size // 2]
     return pl.pallas_call(
-        subtract,
-        grid=(rows // LAST,),
+        functools.partial(subtract, sizes),
         out_shape=jax.ShapeDtypeStruct((rows, cols), F32),
-        in_specs=[
-            pl.BlockSpec((LAST, cols), lambda i: (i, 0)),
-            pl.BlockSpec((LAST, nb * final), lambda i: (i, 0)),
-            pl.BlockSpec((3 * nb * final, cols), lambda i: (0, 0)),
+        in_specs=[anywhere] * 3,
+        out_specs=anywhere,
+        scratch_shapes=[
+            pltpu.VMEM((rows, cols), F32),
+            pltpu.VMEM((rows, nb * final), F32),
+            pltpu.VMEM((2 * nb * final, cols), BF16),
+            sems((len(sizes),)), sems((len(sizes),)), sems, sems((len(sizes),)),
         ],
-        out_specs=pl.BlockSpec((LAST, cols), lambda i: (i, 0)),
+        compiler_params=pltpu.CompilerParams(vmem_limit_bytes=VMEM_BYTES),
     )(early, basis, scaled)
 
 

time: 319 us -> 312 us (0.978)
  Pallas kernels: 319 us -> 312 us
    pallas_call x1, Pallas kernels: 19.8 us -> 15.8 us  [shards(): pl.pallas_call(functools.partial(subtract, sizes), out_shape=jax.ShapeDty...]
where the time goes in v3:
time: 312 us
  Pallas kernels  312 us (100%)
    pallas_call x1, Pallas kernels, shards(): pl.pallas_call(functools.partial(kernel, n, g, plan), out_shape=(jax.Shap...  296 us
    pallas_call x1, Pallas kernels, shards(): pl.pallas_call(functools.partial(subtract, sizes), out_shape=jax.ShapeDty...  15.8 us

profile of v3, /device:TPU:0, one launch (start us, length us, event | category | flops | bytes accessed | tf_op | source)
XLA Modules:
  0.0 312.2 jit_solution(14087867242346982181)
XLA Ops:
  0.0 296.2 %shard_map.37 = (f32[4096,1024]{1,0:T(8,128)}, f32[4096,384]{1,0:T(8,128)}, bf16[768,1024]{1,0:T(8,128)(2,1)}) custom-call(f32[4096,1024]{1,0:T(8,128)} %x_in.1, f32[2,4096,128]{2,1,0:T(8,128)} %v_in.1, f32[2,128,128]{2,1,0:T(8,128)} %t_in.1), custom_call_target="tpu_custom_call" | custom-call | tf_op jit(solution)/shard_map/pallas_call | solution.py:515
  296.2 15.8 %shard_map.38 = f32[4096,1024]{1,0:T(8,128)} custom-call(f32[4096,1024]{1,0:T(8,128)} %get-tuple-element.8.x_in, f32[4096,384]{1,0:T(8,128)} %get-tuple-element.9.v_in, bf16[768,1024]{1,0:T(8,128)(2,1)} %get-tuple-element.10.y_in), custom_call_target="tpu_custom_call" | custom-call | tf_op jit(solution)/shard_map/pallas_call | solution.py:548
